TPU v7x, 256 devices: a whole 4x4x8 slice. The times are simulated.
256 devices in a mesh: ao: 32 (over x_lo, z, core), gen: 4 (over y), act: 2 (over x_hi).
Axes of the slice: x: 4 (x_hi: 2, x_lo: 2; x = x_hi * 2 + x_lo), y: 4, z: 8, core: 2. Of those that a mesh axis runs over, the one named last changes fastest.
Arguments:
- integrals: bfloat16 [3072, 2, 128, 1152], P(('ao', 'gen', 'act')), may hold values from -24 to 24
- bra_rows: bfloat16 [3072, 2, 128, 16], P(('ao', 'gen', 'act')), may hold values from -0.009765625 to 0.009765625
- ket_rows: bfloat16 [3072, 2, 128, 48], P(('ao', 'gen', 'act')), may hold values from -6 to 6
- block_count: int32 [256], P(('ao', 'gen', 'act')), may hold values from 1 to 12, as said below
- pair_count: int32 [3072], P(('ao', 'gen', 'act')), may hold values from 32 to 128
Outputs:
- transformed: float32 [2, 16, 48, 1152], P(None, 'gen', 'act', 'ao')
Inputs may be any that keep to these rules, and one draw needn't show every extreme that they name: `block_count`: one device holds exactly 12 live blocks. Rows from pair_count on are padding.
All inputs are finite; a program needn't handle non-finite values.
Results may differ from a plain program's by a relative error of at most 0.0042.
Values may be sent and summed in bfloat16 or wider, within the bound.
A program may use at most 128 MiB of HBM per device.

v0:
```python
import jax
import jax.numpy as jnp
from jax import lax
from jax.sharding import PartitionSpec as P


def cut_along(array, dim, size):
    lengths = array.shape
    parts = array.reshape(*lengths[:dim], size, lengths[dim] // size, *lengths[dim + 1 :])
    return jnp.moveaxis(parts, dim, 0)


def summed_on_arrival(array, axis, dim):
    parts = cut_along(array, dim, lax.axis_size(axis))
    arrived = lax.all_to_all(parts, axis, split_axis=0, concat_axis=0, tiled=True)
    return arrived.astype(jnp.float32).sum(axis=0)


def sent_and_summed(array, axis, dim):
    parts = cut_along(array, dim, lax.axis_size(axis))
    arrived = lax.all_to_all(parts, axis, split_axis=0, concat_axis=0, tiled=True)
    return arrived.sum(axis=0)


def block_product(ints_block, bra_block, ket_block):
    bra_wide = bra_block.astype(jnp.float32)
    ket_wide = ket_block.astype(jnp.float32)
    real_part = (
        bra_wide[0][:, :, None] * ket_wide[0][:, None, :]
        + bra_wide[1][:, :, None] * ket_wide[1][:, None, :]
    )
    imag_part = (
        bra_wide[0][:, :, None] * ket_wide[1][:, None, :]
        - bra_wide[1][:, :, None] * ket_wide[0][:, None, :]
    )
    rows = bra_block.shape[1]
    real_low = real_part.reshape(rows, -1).T.astype(jnp.bfloat16)
    imag_low = imag_part.reshape(rows, -1).T.astype(jnp.bfloat16)
    upper = jnp.concatenate([real_low, -imag_low], axis=1)
    lower = jnp.concatenate([imag_low, real_low], axis=1)
    weights = jnp.concatenate([upper, lower], axis=0)
    stacked = ints_block.reshape(2 * rows, -1)
    return jnp.dot(weights, stacked, preferred_element_type=jnp.float32)


def local(integrals, bra_rows, ket_rows, block_count, pair_count):
    blocks = integrals.shape[0]
    pair_width = integrals.shape[2]
    columns = integrals.shape[3]
    general = bra_rows.shape[3]
    active = ket_rows.shape[3]
    pair_mask = (jnp.arange(pair_width, dtype=jnp.int32)[None, :] < pair_count[:, None]).astype(
        jnp.bfloat16
    )
    block_live = (jnp.arange(blocks, dtype=jnp.int32) < block_count[0]).astype(jnp.bfloat16)
    masked_ket = ket_rows * pair_mask[:, None, :, None] * block_live[:, None, None, None]
    init = jnp.zeros((2 * general * active, columns), jnp.float32)

    def accumulate(step_number, totals):
        ints_block = lax.dynamic_index_in_dim(integrals, step_number, 0, keepdims=False)
        bra_block = lax.dynamic_index_in_dim(bra_rows, step_number, 0, keepdims=False)
        ket_block = lax.dynamic_index_in_dim(masked_ket, step_number, 0, keepdims=False)
        return totals + block_product(ints_block, bra_block, ket_block)

    totals = lax.fori_loop(0, block_count[0], accumulate, init)
    partial_value = totals.reshape(2, general, active, columns)
    reduced = summed_on_arrival(partial_value.astype(jnp.bfloat16), "ao", 3)
    reduced = sent_and_summed(reduced, "gen", 1)
    reduced = sent_and_summed(reduced, "act", 2)
    return reduced


def solution(mesh):
    in_specs = (
        P(("ao", "gen", "act"), None, None, None),
        P(("ao", "gen", "act"), None, None, None),
        P(("ao", "gen", "act"), None, None, None),
        P(("ao", "gen", "act")),
        P(("ao", "gen", "act")),
    )
    out_specs = P(None, "gen", "act", "ao")
    return jax.shard_map(local, mesh=mesh, in_specs=in_specs, out_specs=out_specs, check_vma=False)
```

profile of v0, /device:TPU:1, one launch (start us, length us, event | category | flops | bytes accessed | tf_op | source)
XLA Modules:
  0.0 305.6 jit_solution(7838419541100828250)
XLA Ops:
  0.7 0.7 fusion.8
  1.4 1.1 multiply_multiply_fusion
  2.5 3.4 %broadcast_in_dim.2 = f32[1536,1152]{1,0:T(8,128)} broadcast(f32[]{:T(128)} %constant.20.clone.1), dimensions={} | broadcast | bytes 7077892 | tf_op jit(solution)/shard_map/broadcast_in_dim | solution.py:57
  5.8 20.3 %while.10 = (s32[]{:T(128)}, f32[1536,1152]{1,0:T(8,128)}, s32[]{:T(128)}, bf16[12,2,128,16]{2,3,1,0:T(8,128)(2,1)}, bf16[12,2,128,48]{2,3,1,0:T(8,128)(2,1)S(1)...) while((s32[]{:T(128)}, f32[1536,1152]{1,0:T(8,128)}, s32[]{:T(128)}, ...), condition=%wide.region_1.2_spmd, body=%wide.region_0.1_spmd.sunk | while | flops 911785984 | bytes 17596564 | solution.py:65
  6.5 1.1 constant_dynamic-slice_fusion.2
  7.6 0.7 dynamic-slice_convert_fusion.5
  8.4 0.1 subtract_convert_fusion.2
  8.5 7.1 %convolution_add_fusion.2 = f32[1536,1152]{1,0:T(8,128)} fusion(f32[1536,1152]{1,0:T(8,128)} %get-tuple-element.117, bf16[256,1152]{1,0:T(8,128)(2,1)S(1)} %bitcast.55, bf16[768,128]{1,0:T(8,128)(2,1)S(1)} %bitcast.57, bf16[768,128]{1,0:T(8,128)(2,1)S(1)} %bitcast.56, bf16[768,128]{1,0:T(8,128)(2,1)S(1)} %bitcast_negate_fusion.2), kind=kOutput, calls=%fused_computation.clone.1 | convolution fusion | flops 910884864 | bytes 15335424 | tf_op jit(solution)/shard_map/while/body/dot_general | solution.py:43
  16.3 1.1 constant_dynamic-slice_fusion.2
  17.4 0.7 dynamic-slice_convert_fusion.5
  18.2 0.1 subtract_convert_fusion.2
  18.3 7.1 %convolution_add_fusion.2 = f32[1536,1152]{1,0:T(8,128)} fusion(f32[1536,1152]{1,0:T(8,128)} %get-tuple-element.117, bf16[256,1152]{1,0:T(8,128)(2,1)S(1)} %bitcast.55, bf16[768,128]{1,0:T(8,128)(2,1)S(1)} %bitcast.57, bf16[768,128]{1,0:T(8,128)(2,1)S(1)} %bitcast.56, bf16[768,128]{1,0:T(8,128)(2,1)S(1)} %bitcast_negate_fusion.2), kind=kOutput, calls=%fused_computation.clone.1 | convolution fusion | flops 910884864 | bytes 15335424 | tf_op jit(solution)/shard_map/while/body/dot_general | solution.py:43
  26.1 5.2 %convert_element_type.52 = bf16[1536,1152]{1,0:T(8,128)(2,1)} convert(f32[1536,1152]{1,0:T(8,128)} %get-tuple-element.38) | non-fusion elementwise | flops 1769472 | bytes 10616832 | tf_op jit(solution)/shard_map/convert_element_type | solution.py:67
  31.3 4.4 %copy.15 = bf16[1536,1152]{0,1:T(8,128)(2,1)S(1)} copy(bf16[1536,1152]{1,0:T(8,128)(2,1)} %convert_element_type.52) | data formatting | bytes 7077888 | tf_op jit(solution)/shard_map/convert_element_type | solution.py:67
  35.7 11.0 %convert_element_type.53 = bf16[2,16,48,32,36]{2,1,0,4,3:T(8,128)(2,1)} reshape(bf16[1536,1152]{0,1:T(8,128)(2,1)S(1)} %copy.15) | data formatting | bytes 7077888 | tf_op jit(solution)/shard_map/convert_element_type | solution.py:67
  46.7 9.9 %bitcast_bitcast_fusion = bf16[32,36,2,16,48]{4,3,2,1,0:T(8,128)(2,1)} fusion(bf16[2,16,48,32,36]{2,1,0,4,3:T(8,128)(2,1)} %convert_element_type.53), kind=kLoop, calls=%fused_computation.25 | loop fusion | bytes 7077888
  56.6 19.4 %reshape.74 = bf16[32,2,27648]{2,1,0:T(2,128)(2,1)S(1)} reshape(bf16[32,36,2,16,48]{4,3,2,1,0:T(8,128)(2,1)} %bitcast_bitcast_fusion) | data formatting | bytes 7077888
  76.1 140.4 %all_to_all.15 = bf16[32,2,27648]{2,1,0:T(2,128)(2,1)} all-to-all(bf16[32,2,27648]{2,1,0:T(2,128)(2,1)S(1)} %reshape.74), channel_id=1, replica_groups=mesh['ao'=32,'gen'=4,'act'=2] {'ao'}, dimensions={0} | all-to-all | bytes 7077888 | tf_op jit(solution)/shard_map/all_to_all | solution.py:15
  216.5 14.0 %reshape.75 = bf16[32,36,2,16,48]{4,3,2,1,0:T(8,128)(2,1)} reshape(bf16[32,2,27648]{2,1,0:T(2,128)(2,1)} %all_to_all.15) | data formatting | bytes 7077888
  230.5 5.6 %convert_reduce_fusion = f32[2,16,48,36]{2,1,0,3:T(8,128)S(1)} fusion(bf16[32,36,2,16,48]{4,3,2,1,0:T(8,128)(2,1)} %reshape.75), kind=kLoop, calls=%fused_computation.19 | loop fusion | flops 3483648 | bytes 3760128 | tf_op jit(solution)/shard_map/reduce_sum | solution.py:16
  236.1 0.1 copy.22
  236.2 0.6 reshape.76
  236.9 57.3 %all_to_all.16 = f32[4,1,13824]{2,1,0:T(1,128)S(1)} all-to-all(f32[4,1,13824]{2,1,0:T(1,128)S(1)} %reshape.76), channel_id=1, replica_groups=mesh['ao'=32,'gen'=4,'act'=2] {'gen'}, dimensions={0} | all-to-all | bytes 442368 | tf_op jit(solution)/shard_map/all_to_all | solution.py:21
  294.2 0.5 broadcast.25
  294.7 1.3 reduce
  296.0 0.6 reshape.77
  296.6 0.1 bitcast_reduce_fusion
  296.7 0.1 copy.17
  296.8 0.2 reshape.78
  297.0 6.8 %all_to_all.17 = f32[2,1,6912]{2,1,0:T(1,128)S(1)} all-to-all(f32[2,1,6912]{2,1,0:T(1,128)S(1)} %reshape.78), channel_id=1, replica_groups=mesh['ao'=32,'gen'=4,'act'=2] {'act'}, dimensions={0} | all-to-all | bytes 110592 | tf_op jit(solution)/shard_map/all_to_all | solution.py:21
  303.8 0.8 reduce.1
  304.6 0.2 reshape.79
  304.9 0.7 reduce_sum.29
  (10 shorter events, 0.2 us)
where the time goes:
time: 310 us; the launch traced here: 306 us
  blocking collectives  205 us (66%)
  local copies, waits for them, and re-layouts  66.9 us (22%)
  other arithmetic  17.1 us (6%)
  matrix products  14.2 us (5%)
    all_to_all x1, blocking collectives, summed_on_arrival(): lax.all_to_all(parts, axis, split_axis=0, concat_axis=0, tiled=True)  140 us
    all_to_all x2, blocking collectives, sent_and_summed(): lax.all_to_all(parts, axis, split_axis=0, concat_axis=0, tiled=True)  64.1 us
    unnamed x7, local copies, waits for them, and re-layouts  45.1 us
    convert_element_type x2, local copies, waits for them, and re-layouts, local(): reduced = summed_on_arrival(partial_value.astype(jnp.bfloat16), 'ao', 3)  15.4 us
    dot_general x2, matrix products, block_product(): return jnp.dot(weights, stacked, preferred_element_type=jnp.float32)  14.2 us

commit v1 on v0

v1 whole, which is shorter than its diff:
```python
import jax
import jax.numpy as jnp
from jax import lax
from jax.experimental import pallas as pl
from jax.experimental.pallas import tpu as pltpu
from jax.sharding import PartitionSpec as P

MESH = pl.DeviceIdType.MESH
NBLK = 12
DEPTH = 256
VW = 1152
ROWS = 96
WIDE = 640
MSG = 48


def kernel(ints_hbm, bra_ref, ket_ref, block_count, pair_count, out_ref,
           ints, weights, psend, precv, s1, r1, s2, r2, turned, s3, r3,
           load_sem, p_send, p_recv, s1_send, s1_recv, s2_send, s2_recv, s3_send, s3_recv):
    ao, gen, act = lax.axis_index("ao"), lax.axis_index("gen"), lax.axis_index("act")
    core = ao % 2
    z = (ao // 2) % 8
    x_lo = ao // 16
    x_hi = act
    x = 2 * x_hi + x_lo
    y = gen

    def device(xx, yy, zz, cc):
        return (((xx % 2) * 8 + zz) * 2 + cc, yy, xx // 2)

    def first(d):
        return device(core * x + (1 - core) * d, core * d + (1 - core) * y, z, core)

    def second(d):
        return device(core * d + (1 - core) * x, core * y + (1 - core) * d, z, core)

    me1 = (1 - core) * x + core * y
    me2 = (1 - core) * y + core * x

    loads = []
    for b in range(NBLK):
        rows = pl.ds(b * DEPTH, DEPTH)
        loads.append(pltpu.make_async_copy(ints_hbm.at[rows], ints.at[rows], load_sem.at[b]))
        loads[-1].start()

    barrier = pltpu.get_barrier_semaphore()
    pl.semaphore_signal(barrier, inc=1, device_id=device(x, y, z, 1 - core), device_id_type=MESH)
    for k in (1, 2, 3):
        pl.semaphore_signal(barrier, inc=1, device_id=first((me1 + k) % 4), device_id_type=MESH)
        pl.semaphore_signal(barrier, inc=1, device_id=second((me2 + k) % 4), device_id_type=MESH)
    for k in range(1, 8):
        for c in (0, 1):
            pl.semaphore_signal(barrier, inc=1, device_id=device(x, y, (z + k) % 8, c), device_id_type=MESH)

    lane = lax.broadcasted_iota(jnp.int32, (48, 128), 1)
    eye16 = (lax.broadcasted_iota(jnp.int32, (16, 16), 0) == lax.broadcasted_iota(jnp.int32, (16, 16), 1)).astype(jnp.bfloat16)
    eye48 = (lax.broadcasted_iota(jnp.int32, (48, 48), 0) == lax.broadcasted_iota(jnp.int32, (48, 48), 1)).astype(jnp.bfloat16)

    def flipped(eye, block):
        return lax.dot_general(eye, block, (((1,), (1,)), ((), ())), preferred_element_type=jnp.float32)

    live_blocks = block_count[0]

    def build(b, carry):
        live = jnp.where(b < live_blocks, pair_count[b], 0)
        keep = lane < live
        bra_re = flipped(eye16, bra_ref[b, 0])
        bra_im = flipped(eye16, bra_ref[b, 1])
        ket_re = jnp.where(keep, flipped(eye48, ket_ref[b, 0]), 0.0)
        ket_im = jnp.where(keep, flipped(eye48, ket_ref[b, 1]), 0.0)
        low = pl.ds(pl.multiple_of(b * DEPTH, DEPTH), 128)
        high = pl.ds(pl.multiple_of(b * DEPTH + 128, 128), 128)
        for xh in (0, 1):
            kr = ket_re[xh * 24 : xh * 24 + 24]
            ki = ket_im[xh * 24 : xh * 24 + 24]
            for yy in range(4):
                re, im = [], []
                for p in range(4):
                    br = bra_re[yy * 4 + p : yy * 4 + p + 1]
                    bi = bra_im[yy * 4 + p : yy * 4 + p + 1]
                    re.append(br * kr + bi * ki)
                    im.append(br * ki - bi * kr)
                re = jnp.concatenate(re, axis=0)
                im = jnp.concatenate(im, axis=0)
                re_low = re.astype(jnp.bfloat16)
                im_low = im.astype(jnp.bfloat16)
                weights[0, xh * 4 + yy, :, low] = re_low
                weights[0, xh * 4 + yy, :, high] = -im_low
                weights[1, yy * 2 + xh, :, low] = im_low
                weights[1, yy * 2 + xh, :, high] = re_low
        return carry

    lax.fori_loop(0, NBLK, build, 0)

    for copy in loads:
        copy.wait()

    other_x = 1 - x_hi

    def chunk_of(part, t):
        from_x = (other_x if t < 2 else x_hi) * 2 + t % 2
        from_y = (y + (2, 1, 3, 0)[t]) % 4
        return (1 - part) * from_x + part * from_y

    def product(part, chunk):
        lhs = weights[part, pl.ds(chunk * 2, 2)].reshape(2 * ROWS, NBLK * DEPTH)
        return jnp.dot(lhs, ints[...], preferred_element_type=jnp.float32)

    def p_copy(t):
        return pltpu.make_async_remote_copy(
            src_ref=psend.at[t], dst_ref=precv.at[t], send_sem=p_send.at[t], recv_sem=p_recv.at[t],
            device_id=device(x, y, z, 1 - core), device_id_type=MESH)

    def for_partner(t):
        psend[t] = product(1 - core, chunk_of(1 - core, t)).astype(jnp.bfloat16)
        if t == 0:
            pl.semaphore_wait(barrier, 21)
        p_copy(t).start()

    def s1_target(t, a):
        d1 = (1 - core) * (2 * (other_x if t < 2 else x_hi) + a) + core * chunk_of(1, t)
        half = (1 - core) * (t % 2) + core * a
        return d1, half

    def s1_copy(t, a):
        d1, half = s1_target(t, a)
        slot = (me1 - d1 + 7) % 4
        return pltpu.make_async_remote_copy(
            src_ref=s1.at[d1, half], dst_ref=r1.at[slot % 3, half],
            send_sem=s1_send.at[t, a], recv_sem=s1_recv.at[slot % 3, half],
            device_id=first(d1), device_id_type=MESH)

    def for_self(t):
        value = product(core, chunk_of(core, t))
        p_copy(t).wait_recv()
        value = value + precv[t].astype(jnp.float32)
        low = value.astype(jnp.bfloat16)
        for j in (0, 1):
            for xl in (0, 1):
                d1 = (1 - core) * (2 * (other_x if t < 2 else x_hi) + xl) + core * chunk_of(1, t)
                d2 = (1 - core) * (2 * (t % 2) + j) + core * (2 * j + xl)
                s1[d1, d2 // 2, d2 % 2] = low[j * ROWS : (j + 1) * ROWS, xl * 512 : xl * 512 + WIDE]
        for a in (0, 1):
            d1, _ = s1_target(t, a)

            @pl.when(d1 != me1)
            def _():
                s1_copy(t, a).start()

    for_partner(0)
    for_partner(1)
    for_self(0)
    for_partner(2)
    for_self(1)
    for_partner(3)
    for_self(2)
    for_self(3)

    def s1_arrival(slot, half):
        return pltpu.make_async_remote_copy(
            src_ref=s1.at[0, half], dst_ref=r1.at[slot, half],
            send_sem=s1_send.at[0, 0], recv_sem=s1_recv.at[slot, half],
            device_id=first((me1 + 1) % 4), device_id_type=MESH)

    for slot in range(3):
        for half in (0, 1):
            s1_arrival(slot, half).wait_recv()

    def s2_copy(k):
        d2 = (me2 + k) % 4
        slot = 3 - k
        return pltpu.make_async_remote_copy(
            src_ref=s2.at[k - 1], dst_ref=r2.at[slot], send_sem=s2_send.at[k - 1], recv_sem=s2_recv.at[slot],
            device_id=second(d2), device_id_type=MESH)

    def summed(d2):
        half, side = d2 // 2, d2 % 2
        total = s1[me1, half, side].astype(jnp.float32)
        for slot in range(3):
            total = total + r1[slot, half, side].astype(jnp.float32)
        return total

    for k in (2, 1, 3):
        s2[k - 1] = summed((me2 + k) % 4).astype(jnp.bfloat16)
        s2_copy(k).start()
    total = summed(me2)
    for k in (1, 2, 3):
        s2_copy(k).wait_recv()
        total = total + r2[3 - k].astype(jnp.float32)

    pad = jnp.zeros((32, 128), jnp.float32)
    for tile in range(5):
        turned[tile * 128 : (tile + 1) * 128] = jnp.concatenate([total[:, tile * 128 : (tile + 1) * 128], pad], axis=0).T
    turned[WIDE:] = jnp.zeros((16, 128), jnp.float32)

    def s3_copy(k, c):
        zz = (z + k) % 8
        return pltpu.make_async_remote_copy(
            src_ref=s3.at[zz, c], dst_ref=r3.at[core, z], send_sem=s3_send.at[k, c], recv_sem=s3_recv.at[core, z],
            device_id=device(x, y, zz, c), device_id_type=MESH)

    for k in (4, 3, 5, 2, 6, 1, 7, 0):
        zz = (z + k) % 8
        for c in (0, 1):
            start = pl.multiple_of(64 * x_lo + 72 * zz + 32 * c, 8)
            s3[zz, c] = turned[pl.ds(start, MSG)].astype(jnp.bfloat16)
            if k > 0:
                s3_copy(k, c).start()
            else:

                @pl.when(core != c)
                def _():
                    s3_copy(k, c).start()

    r3[core, z] = s3[z, core]
    for k in range(8):
        zz = (z + k) % 8
        for c in (0, 1):

            def arrival():
                return pltpu.make_async_remote_copy(
                    src_ref=s3.at[0, 0], dst_ref=r3.at[c, zz], send_sem=s3_send.at[0, 0], recv_sem=s3_recv.at[c, zz],
                    device_id=device(x, y, z, 1 - core), device_id_type=MESH)

            if k > 0:
                arrival().wait_recv()
            else:

                @pl.when(core != c)
                def _():
                    arrival().wait_recv()

    fill = jnp.zeros((128 - MSG, 128), jnp.float32)
    for r in (0, 1):
        piece = r3[r, 0].astype(jnp.float32)
        for zz in range(1, 8):
            piece = piece + r3[r, zz].astype(jnp.float32)
        back = jnp.concatenate([piece, fill], axis=0).T
        out_ref[r] = jnp.where(core == 0, back[:ROWS, :36], back[:ROWS, 4:40])

    for t in range(4):
        p_copy(t).wait_send()
        for a in (0, 1):
            d1, _ = s1_target(t, a)

            @pl.when(d1 != me1)
            def _():
                s1_copy(t, a).wait_send()
    for k in (1, 2, 3):
        s2_copy(k).wait_send()
    for k in range(8):
        for c in (0, 1):
            if k > 0:
                s3_copy(k, c).wait_send()
            else:

                @pl.when(core != c)
                def _():
                    s3_copy(k, c).wait_send()


def local(integrals, bra_rows, ket_rows, block_count, pair_count):
    bf16, f32 = jnp.bfloat16, jnp.float32
    out = pl.pallas_call(
        kernel,
        out_shape=jax.ShapeDtypeStruct((2, ROWS, 36), f32),
        in_specs=[
            pl.BlockSpec(memory_space=pl.ANY),
            pl.BlockSpec(memory_space=pltpu.VMEM),
            pl.BlockSpec(memory_space=pltpu.VMEM),
            pl.BlockSpec(memory_space=pltpu.SMEM),
            pl.BlockSpec(memory_space=pltpu.SMEM),
        ],
        out_specs=pl.BlockSpec(memory_space=pltpu.VMEM),
        scratch_shapes=[
            pltpu.VMEM((NBLK * DEPTH, VW), bf16),
            pltpu.VMEM((2, 8, ROWS, NBLK * DEPTH), bf16),
            pltpu.VMEM((4, 2 * ROWS, VW), bf16),
            pltpu.VMEM((4, 2 * ROWS, VW), bf16),
            pltpu.VMEM((4, 2, 2, ROWS, WIDE), bf16),
            pltpu.VMEM((3, 2, 2, ROWS, WIDE), bf16),
            pltpu.VMEM((3, ROWS, WIDE), bf16),
            pltpu.VMEM((3, ROWS, WIDE), bf16),
            pltpu.VMEM((WIDE + 16, 128), f32),
            pltpu.VMEM((8, 2, MSG, 128), bf16),
            pltpu.VMEM((2, 8, MSG, 128), bf16),
            pltpu.SemaphoreType.DMA((NBLK,)),
            pltpu.SemaphoreType.DMA((4,)),
            pltpu.SemaphoreType.DMA((4,)),
            pltpu.SemaphoreType.DMA((4, 2)),
            pltpu.SemaphoreType.DMA((3, 2)),
            pltpu.SemaphoreType.DMA((3,)),
            pltpu.SemaphoreType.DMA((3,)),
            pltpu.SemaphoreType.DMA((8, 2)),
            pltpu.SemaphoreType.DMA((2, 8)),
        ],
        compiler_params=pltpu.CompilerParams(
            collective_id=0, has_side_effects=True, vmem_limit_bytes=56 * 1024 * 1024
        ),
        name="transform",
    )(integrals.reshape(NBLK * DEPTH, VW), bra_rows, ket_rows, block_count, pair_count)
    return out.reshape(2, 4, 24, 36)


def solution(mesh):
    split = ("ao", "gen", "act")
    in_specs = (
        P(split, None, None, None),
        P(split, None, None, None),
        P(split, None, None, None),
        P(split),
        P(split),
    )
    out_specs = P(None, "gen", "act", "ao")
    return jax.shard_map(local, mesh=mesh, in_specs=in_specs, out_specs=out_specs, check_vma=False)
```

time: 310 us -> 54.7 us (0.18); the launches traced: 306 us -> 54.5 us
  blocking collectives: 205 us -> 0 us
  local copies, waits for them, and re-layouts: 66.9 us -> 5.73 us
  Pallas kernels: 0 us -> 48.1 us
  other arithmetic: 17.1 us -> 0 us
  matrix products: 14.2 us -> 0 us
    all_to_all x3 -> x0, blocking collectives: 205 us -> none  [the longest x1 140 us: summed_on_arrival(): lax.all_to_all(parts, axis, split_axis=0, concat_axis=0, tiled=True)]
    pallas_call x0 -> x1, Pallas kernels: none -> 48.1 us  [local(): pl.pallas_call(kernel, out_shape=jax.ShapeDtypeStruct((2, ROWS, 36), f32)...]
    unnamed x7 -> x3, local copies, waits for them, and re-layouts: 45.1 us -> 5.73 us
    convert_element_type x2 -> x0, local copies, waits for them, and re-layouts: 15.4 us -> none  [local(): reduced = summed_on_arrival(partial_value.astype(jnp.bfloat16), 'ao', 3)]
    dot_general x2 -> x0, matrix products: 14.2 us -> none  [block_product(): return jnp.dot(weights, stacked, preferred_element_type=jnp.float32)]
    convert_element_type x9 -> x0, other arithmetic: 7.58 us -> none  [the longest x1 5.19 us: local(): reduced = summed_on_arrival(partial_value.astype(jnp.bfloat16), 'ao', 3)]
    reduce_sum x3 -> x0, other arithmetic: 6.37 us -> none  [the longest x1 5.6 us: summed_on_arrival(): return arrived.astype(jnp.float32).sum(axis=0)]
    broadcast_in_dim x1 -> x0, local copies, waits for them, and re-layouts: 3.37 us -> none  [local(): init = jnp.zeros((2 * general * active, columns), jnp.float32)]
where the time goes in v1:
time: 54.7 us; the launch traced here: 54.5 us
  Pallas kernels  48.1 us (88%)
  local copies, waits for them, and re-layouts  5.73 us (10%)
  between operations  0.66 us (1%)
    pallas_call x1, Pallas kernels, local(): pl.pallas_call(kernel, out_shape=jax.ShapeDtypeStruct((2, ROWS, 36), f32)...  48.1 us
    unnamed x3, local copies, waits for them, and re-layouts  5.73 us

profile of v1, /device:TPU:1, one launch (start us, length us, event | category | flops | bytes accessed | tf_op | source)
XLA Modules:
  0.0 54.5 jit_solution(18346862977044988096)
XLA Ops:
  0.7 2.0 %copy.6.bra_ref = bf16[12,2,128,16]{3,2,1,0:T(8,128)(2,1)} copy(bf16[12,2,128,16]{2,3,1,0:T(8,128)(2,1)} %param.6) | data formatting | bytes 196608 | tf_op args[1]
  2.7 2.1 %copy.7.ket_ref = bf16[12,2,128,48]{3,2,1,0:T(8,128)(2,1)} copy(bf16[12,2,128,48]{2,3,1,0:T(8,128)(2,1)} %param.7) | data formatting | bytes 589824 | tf_op args[2]
  4.8 48.1 %transform.1 = f32[2,96,36]{2,1,0:T(8,128)} custom-call(bf16[3072,1152]{1,0:T(8,128)(2,1)} %bitcast.2, bf16[12,2,128,16]{3,2,1,0:T(8,128)(2,1)} %copy.6.bra_ref, bf16[12,2,128,48]{3,2,1,0:T(8,128)(2,1)} %copy.7.ket_ref, s32[1]{0:T(128)S(6)} %copy.9.block_count, s32[12]{0:T(128)} %pair_count.1), custom_call_target="tpu_custom_call" | custom-call | tf_op jit(solution)/shard_map/transform/pallas_call | solution.py:264
  53.0 1.5 %copy.10 = f32[2,4,24,36]{3,2,1,0:T(8,128)} copy(f32[2,4,24,36]{3,2,1,0:T(8,128)} %bitcast.3) | data formatting | bytes 55296

commit v2 on v1

--- a/solution.py
+++ b/solution.py
@@ -15,7 +15,7 @@
 
 
 def kernel(ints_hbm, bra_ref, ket_ref, block_count, pair_count, out_ref,
-           ints, weights, psend, precv, s1, r1, s2, r2, turned, s3, r3,
+           ints, bra_wide, ket_wide, weights, psend, precv, s1, r1, joined, s2, r2, mine, turned, s3, r3,
            load_sem, p_send, p_recv, s1_send, s1_recv, s2_send, s2_recv, s3_send, s3_recv):
     ao, gen, act = lax.axis_index("ao"), lax.axis_index("gen"), lax.axis_index("act")
     core = ao % 2
@@ -53,31 +53,24 @@
             pl.semaphore_signal(barrier, inc=1, device_id=device(x, y, (z + k) % 8, c), device_id_type=MESH)
 
     lane = lax.broadcasted_iota(jnp.int32, (48, 128), 1)
-    eye16 = (lax.broadcasted_iota(jnp.int32, (16, 16), 0) == lax.broadcasted_iota(jnp.int32, (16, 16), 1)).astype(jnp.bfloat16)
-    eye48 = (lax.broadcasted_iota(jnp.int32, (48, 48), 0) == lax.broadcasted_iota(jnp.int32, (48, 48), 1)).astype(jnp.bfloat16)
-
-    def flipped(eye, block):
-        return lax.dot_general(eye, block, (((1,), (1,)), ((), ())), preferred_element_type=jnp.float32)
-
     live_blocks = block_count[0]
 
     def build(b, carry):
         live = jnp.where(b < live_blocks, pair_count[b], 0)
         keep = lane < live
-        bra_re = flipped(eye16, bra_ref[b, 0])
-        bra_im = flipped(eye16, bra_ref[b, 1])
-        ket_re = jnp.where(keep, flipped(eye48, ket_ref[b, 0]), 0.0)
-        ket_im = jnp.where(keep, flipped(eye48, ket_ref[b, 1]), 0.0)
+        for r in (0, 1):
+            bra_wide[r] = bra_ref[b, r].astype(jnp.float32)
+            ket_wide[r] = jnp.where(keep, ket_ref[b, r].astype(jnp.float32), 0.0)
         low = pl.ds(pl.multiple_of(b * DEPTH, DEPTH), 128)
         high = pl.ds(pl.multiple_of(b * DEPTH + 128, 128), 128)
         for xh in (0, 1):
-            kr = ket_re[xh * 24 : xh * 24 + 24]
-            ki = ket_im[xh * 24 : xh * 24 + 24]
+            kr = ket_wide[0, xh * 24 : xh * 24 + 24]
+            ki = ket_wide[1, xh * 24 : xh * 24 + 24]
             for yy in range(4):
                 re, im = [], []
                 for p in range(4):
-                    br = bra_re[yy * 4 + p : yy * 4 + p + 1]
-                    bi = bra_im[yy * 4 + p : yy * 4 + p + 1]
+                    br = bra_wide[0, yy * 4 + p : yy * 4 + p + 1]
+                    bi = bra_wide[1, yy * 4 + p : yy * 4 + p + 1]
                     re.append(br * kr + bi * ki)
                     im.append(br * ki - bi * kr)
                 re = jnp.concatenate(re, axis=0)
@@ -117,76 +110,125 @@
             pl.semaphore_wait(barrier, 21)
         p_copy(t).start()
 
-    def s1_target(t, a):
-        d1 = (1 - core) * (2 * (other_x if t < 2 else x_hi) + a) + core * chunk_of(1, t)
-        half = (1 - core) * (t % 2) + core * a
-        return d1, half
-
-    def s1_copy(t, a):
-        d1, half = s1_target(t, a)
-        slot = (me1 - d1 + 7) % 4
+    right, left = (me1 + 1) % 4, (me1 + 3) % 4
+    side = {0: right, 1: left}
+
+    def remote1(src_ref, dst_ref, k, to):
         return pltpu.make_async_remote_copy(
-            src_ref=s1.at[d1, half], dst_ref=r1.at[slot % 3, half],
-            send_sem=s1_send.at[t, a], recv_sem=s1_recv.at[slot % 3, half],
-            device_id=first(d1), device_id_type=MESH)
+            src_ref=src_ref, dst_ref=dst_ref, send_sem=s1_send.at[k], recv_sem=s1_recv.at[k],
+            device_id=first(side[to]), device_id_type=MESH)
+
+    def opposite(to):
+        return remote1(s1.at[(me1 + 2) % 4, to], r1.at[to], to, to)
+
+    def plain(to):
+        return remote1(s1.at[side[to], 1 - to], r1.at[2 + to], 2 + to, to)
+
+    def relayed(to):
+        return remote1(joined.at[to], r1.at[4 + to], 4 + to, to)
+
+    def relay(to):
+        opposite(to).wait_recv()
+        for j in (0, 1):
+            joined[to, j] = (s1[side[to], to, j].astype(jnp.float32) + r1[to, j].astype(jnp.float32)).astype(jnp.bfloat16)
+        relayed(to).start()
 
     def for_self(t):
-        value = product(core, chunk_of(core, t))
         p_copy(t).wait_recv()
-        value = value + precv[t].astype(jnp.float32)
+        value = product(core, chunk_of(core, t)) + precv[t].astype(jnp.float32)
         low = value.astype(jnp.bfloat16)
         for j in (0, 1):
             for xl in (0, 1):
                 d1 = (1 - core) * (2 * (other_x if t < 2 else x_hi) + xl) + core * chunk_of(1, t)
                 d2 = (1 - core) * (2 * (t % 2) + j) + core * (2 * j + xl)
                 s1[d1, d2 // 2, d2 % 2] = low[j * ROWS : (j + 1) * ROWS, xl * 512 : xl * 512 + WIDE]
-        for a in (0, 1):
-            d1, _ = s1_target(t, a)
-
-            @pl.when(d1 != me1)
-            def _():
-                s1_copy(t, a).start()
+
+    is_y = core == 1
+    even = jnp.logical_and(core == 0, x_lo == 0)
+    odd = jnp.logical_and(core == 0, x_lo == 1)
+
+    def when(*conditions):
+        condition = conditions[0]
+        for extra in conditions[1:]:
+            condition = jnp.logical_or(condition, extra)
+        return pl.when(condition)
 
     for_partner(0)
     for_partner(1)
     for_self(0)
+    opposite(0).start()
+
+    @when(is_y)
+    def _():
+        opposite(1).start()
+
+    @when(even)
+    def _():
+        plain(1).start()
+
     for_partner(2)
     for_self(1)
+
+    @when(even, odd)
+    def _():
+        opposite(1).start()
+
+    @when(is_y, odd)
+    def _():
+        plain(0).start()
+        relay(0)
+
     for_partner(3)
     for_self(2)
+
+    @when(is_y, odd)
+    def _():
+        plain(1).start()
+
+    @when(even)
+    def _():
+        relay(0)
+
+    @when(is_y, even)
+    def _():
+        relay(1)
+
     for_self(3)
 
-    def s1_arrival(slot, half):
+    @when(even)
+    def _():
+        plain(0).start()
+
+    @when(odd)
+    def _():
+        relay(1)
+
+    def s2_copy(d2, slot):
         return pltpu.make_async_remote_copy(
-            src_ref=s1.at[0, half], dst_ref=r1.at[slot, half],
-            send_sem=s1_send.at[0, 0], recv_sem=s1_recv.at[slot, half],
-            device_id=first((me1 + 1) % 4), device_id_type=MESH)
+            src_ref=s2.at[d2], dst_ref=r2.at[slot], send_sem=s2_send.at[d2], recv_sem=s2_recv.at[slot],
+            device_id=second(d2), device_id_type=MESH)
+
+    for half in (0, 1):
+        relayed(half).wait_recv()
+        plain(1 - half).wait_recv()
+        for j in (0, 1):
+            d2 = 2 * half + j
+            total = s1[me1, half, j].astype(jnp.float32) + r1[4 + half, j].astype(jnp.float32) + r1[3 - half, j].astype(jnp.float32)
+            s2[d2] = total.astype(jnp.bfloat16)
+
+            @pl.when(d2 == me2)
+            def _():
+                mine[...] = total
+
+            @pl.when(d2 != me2)
+            def _():
+                s2_copy(d2, (me2 - d2 + 7) % 4 % 3).start()
 
     for slot in range(3):
-        for half in (0, 1):
-            s1_arrival(slot, half).wait_recv()
-
-    def s2_copy(k):
-        d2 = (me2 + k) % 4
-        slot = 3 - k
-        return pltpu.make_async_remote_copy(
-            src_ref=s2.at[k - 1], dst_ref=r2.at[slot], send_sem=s2_send.at[k - 1], recv_sem=s2_recv.at[slot],
-            device_id=second(d2), device_id_type=MESH)
-
-    def summed(d2):
-        half, side = d2 // 2, d2 % 2
-        total = s1[me1, half, side].astype(jnp.float32)
-        for slot in range(3):
-            total = total + r1[slot, half, side].astype(jnp.float32)
-        return total
-
-    for k in (2, 1, 3):
-        s2[k - 1] = summed((me2 + k) % 4).astype(jnp.bfloat16)
-        s2_copy(k).start()
-    total = summed(me2)
-    for k in (1, 2, 3):
-        s2_copy(k).wait_recv()
-        total = total + r2[3 - k].astype(jnp.float32)
+        s2_copy(0, slot).wait_recv()
+    total = mine[...]
+    for slot in range(3):
+        total = total + r2[slot].astype(jnp.float32)
 
     pad = jnp.zeros((32, 128), jnp.float32)
     for tile in range(5):
@@ -240,14 +282,16 @@
 
     for t in range(4):
         p_copy(t).wait_send()
-        for a in (0, 1):
-            d1, _ = s1_target(t, a)
-
-            @pl.when(d1 != me1)
-            def _():
-                s1_copy(t, a).wait_send()
-    for k in (1, 2, 3):
-        s2_copy(k).wait_send()
+    for to in (0, 1):
+        opposite(to).wait_send()
+        plain(to).wait_send()
+        relayed(to).wait_send()
+    for d2 in range(4):
+
+        @pl.when(d2 != me2)
+        def _():
+            s2_copy(d2, 0).wait_send()
+
     for k in range(8):
         for c in (0, 1):
             if k > 0:
@@ -274,22 +318,26 @@
         out_specs=pl.BlockSpec(memory_space=pltpu.VMEM),
         scratch_shapes=[
             pltpu.VMEM((NBLK * DEPTH, VW), bf16),
+            pltpu.VMEM((2, 16, 128), f32),
+            pltpu.VMEM((2, 48, 128), f32),
             pltpu.VMEM((2, 8, ROWS, NBLK * DEPTH), bf16),
             pltpu.VMEM((4, 2 * ROWS, VW), bf16),
             pltpu.VMEM((4, 2 * ROWS, VW), bf16),
             pltpu.VMEM((4, 2, 2, ROWS, WIDE), bf16),
-            pltpu.VMEM((3, 2, 2, ROWS, WIDE), bf16),
+            pltpu.VMEM((6, 2, ROWS, WIDE), bf16),
+            pltpu.VMEM((2, 2, ROWS, WIDE), bf16),
+            pltpu.VMEM((4, ROWS, WIDE), bf16),
             pltpu.VMEM((3, ROWS, WIDE), bf16),
-            pltpu.VMEM((3, ROWS, WIDE), bf16),
+            pltpu.VMEM((ROWS, WIDE), f32),
             pltpu.VMEM((WIDE + 16, 128), f32),
             pltpu.VMEM((8, 2, MSG, 128), bf16),
             pltpu.VMEM((2, 8, MSG, 128), bf16),
             pltpu.SemaphoreType.DMA((NBLK,)),
             pltpu.SemaphoreType.DMA((4,)),
             pltpu.SemaphoreType.DMA((4,)),
-            pltpu.SemaphoreType.DMA((4, 2)),
-            pltpu.SemaphoreType.DMA((3, 2)),
-            pltpu.SemaphoreType.DMA((3,)),
+            pltpu.SemaphoreType.DMA((6,)),
+            pltpu.SemaphoreType.DMA((6,)),
+            pltpu.SemaphoreType.DMA((4,)),
             pltpu.SemaphoreType.DMA((3,)),
             pltpu.SemaphoreType.DMA((8, 2)),
             pltpu.SemaphoreType.DMA((2, 8)),
@@ -298,7 +346,7 @@
             collective_id=0, has_side_effects=True, vmem_limit_bytes=56 * 1024 * 1024
         ),
         name="transform",
-    )(integrals.reshape(NBLK * DEPTH, VW), bra_rows, ket_rows, block_count, pair_count)
+    )(integrals.reshape(NBLK * DEPTH, VW), jnp.swapaxes(bra_rows, 2, 3), jnp.swapaxes(ket_rows, 2, 3), block_count, pair_count)
     return out.reshape(2, 4, 24, 36)
 
 

time: 54.7 us -> 46.3 us (0.85)
  the two profiles are of different devices: /device:TPU:1 before, /device:TPU:29 now
where the time goes in v2:
time: 46.3 us; the launch traced here: 46.1 us
  Pallas kernels  43.9 us (95%)
  local copies, waits for them, and re-layouts  1.54 us (3%)
  between operations  0.66 us (1%)
    pallas_call x1, Pallas kernels, local(): pl.pallas_call(kernel, out_shape=jax.ShapeDtypeStruct((2, ROWS, 36), f32)...  43.9 us
    unnamed x1, local copies, waits for them, and re-layouts  1.54 us

profile of v2, /device:TPU:29, one launch (start us, length us, event | category | flops | bytes accessed | tf_op | source)
XLA Modules:
  0.0 46.1 jit_solution(9354210330064311779)
XLA Ops:
  0.7 43.9 %transform.1 = f32[2,96,36]{2,1,0:T(8,128)} custom-call(bf16[3072,1152]{1,0:T(8,128)(2,1)} %bitcast.4, bf16[12,2,16,128]{3,2,1,0:T(8,128)(2,1)} %bitcast.7, bf16[12,2,48,128]{3,2,1,0:T(8,128)(2,1)} %bitcast.6, s32[1]{0:T(128)S(6)} %copy.7.block_count, s32[12]{0:T(128)} %pair_count.1), custom_call_target="tpu_custom_call" | custom-call | tf_op jit(solution)/shard_map/transform/pallas_call | solution.py:308
  44.6 1.5 %copy.8 = f32[2,4,24,36]{3,2,1,0:T(8,128)} copy(f32[2,4,24,36]{3,2,1,0:T(8,128)} %bitcast.5) | data formatting | bytes 55296

commit v3 on v1

v3 whole, which is shorter than its diff:
```python
import jax
import jax.numpy as jnp
from jax import lax
from jax.experimental import pallas as pl
from jax.experimental.pallas import tpu as pltpu
from jax.sharding import PartitionSpec as P

MESH = pl.DeviceIdType.MESH
NBLK = 12
DEPTH = 256
VW = 1152
ROWS = 96
HALF = 48
WIDE = 640
MSG = 48


def kernel(ints_hbm, bra_ref, ket_ref, block_count, pair_count, out_ref,
           ints, bra_wide, ket_wide, weights, psend, precv, s1, r1, joined, s2, r2, mine, turned, s3, r3,
           load_sem, p_send, p_recv, s1_send, s1_recv, s2_send, s2_recv, s3_send, s3_recv):
    ao, gen, act = lax.axis_index("ao"), lax.axis_index("gen"), lax.axis_index("act")
    core = ao % 2
    z = (ao // 2) % 8
    x_lo = ao // 16
    x_hi = act
    x = 2 * x_hi + x_lo
    y = gen

    def device(xx, yy, zz, cc):
        return (((xx % 2) * 8 + zz) * 2 + cc, yy, xx // 2)

    def first(d):
        return device(core * x + (1 - core) * d, core * d + (1 - core) * y, z, core)

    def second(d):
        return device(core * d + (1 - core) * x, core * y + (1 - core) * d, z, core)

    me1 = (1 - core) * x + core * y
    me2 = (1 - core) * y + core * x

    loads = []
    for b in range(NBLK):
        rows = pl.ds(b * DEPTH, DEPTH)
        loads.append(pltpu.make_async_copy(ints_hbm.at[rows], ints.at[rows], load_sem.at[b]))
        loads[-1].start()

    barrier = pltpu.get_barrier_semaphore()
    pl.semaphore_signal(barrier, inc=1, device_id=device(x, y, z, 1 - core), device_id_type=MESH)
    for k in (1, 2, 3):
        pl.semaphore_signal(barrier, inc=1, device_id=first((me1 + k) % 4), device_id_type=MESH)
        pl.semaphore_signal(barrier, inc=1, device_id=second((me2 + k) % 4), device_id_type=MESH)
    for k in range(1, 8):
        for c in (0, 1):
            pl.semaphore_signal(barrier, inc=1, device_id=device(x, y, (z + k) % 8, c), device_id_type=MESH)

    lane = lax.broadcasted_iota(jnp.int32, (48, 128), 1)
    live_blocks = block_count[0]

    def build(b, carry):
        live = jnp.where(b < live_blocks, pair_count[b], 0)
        keep = lane < live
        for r in (0, 1):
            bra_wide[r] = bra_ref[b, r].astype(jnp.float32)
            ket_wide[r] = jnp.where(keep, ket_ref[b, r].astype(jnp.float32), 0.0)
        low = pl.ds(pl.multiple_of(b * DEPTH, DEPTH), 128)
        high = pl.ds(pl.multiple_of(b * DEPTH + 128, 128), 128)
        for xh in (0, 1):
            kr = ket_wide[0, xh * 24 : xh * 24 + 24]
            ki = ket_wide[1, xh * 24 : xh * 24 + 24]
            for yy in range(4):
                for ab in (0, 1):
                    re, im = [], []
                    for p in (2 * ab, 2 * ab + 1):
                        br = bra_wide[0, yy * 4 + p : yy * 4 + p + 1]
                        bi = bra_wide[1, yy * 4 + p : yy * 4 + p + 1]
                        re.append(br * kr + bi * ki)
                        im.append(br * ki - bi * kr)
                    re_low = jnp.concatenate(re, axis=0).astype(jnp.bfloat16)
                    im_low = jnp.concatenate(im, axis=0).astype(jnp.bfloat16)
                    rows_x = pl.ds((yy % 2) * HALF, HALF)
                    rows_y = pl.ds(xh * HALF, HALF)
                    weights[0, ab, xh * 2 + yy // 2, rows_x, low] = re_low
                    weights[0, ab, xh * 2 + yy // 2, rows_x, high] = -im_low
                    weights[1, ab, yy, rows_y, low] = im_low
                    weights[1, ab, yy, rows_y, high] = re_low
        return carry

    lax.fori_loop(0, NBLK, build, 0)

    for copy in loads:
        copy.wait()

    to1 = 1 - me1 % 2
    to2 = 1 - to1

    def side(to):
        return (me1 + 1 + 2 * to) % 4

    def groups(part, sub):
        from_x = 2 * (x_hi if sub else 1 - x_hi)
        near = (y + 1 + 2 * (1 - y % 2)) % 4
        far = (y + 1 + 2 * (y % 2)) % 4
        from_y = (far, y) if sub else ((y + 2) % 4, near)
        return [(1 - part) * (from_x + j) + part * from_y[j] for j in (0, 1)]

    def product(part, ab, sub):
        lhs = jnp.concatenate([weights[part, ab, g] for g in groups(part, sub)], axis=0)
        return jnp.dot(lhs, ints[...], preferred_element_type=jnp.float32)

    def p_copy(ab, sub):
        k = 2 * ab + sub
        return pltpu.make_async_remote_copy(
            src_ref=psend.at[k], dst_ref=precv.at[k], send_sem=p_send.at[k], recv_sem=p_recv.at[k],
            device_id=device(x, y, z, 1 - core), device_id_type=MESH)

    def for_partner(ab, sub):
        psend[2 * ab + sub] = product(1 - core, ab, sub).astype(jnp.bfloat16)
        if ab == 0 and sub == 0:
            pl.semaphore_wait(barrier, 21)
        p_copy(ab, sub).start()

    def for_self(ab, sub):
        p_copy(ab, sub).wait_recv()
        value = product(core, ab, sub) + precv[2 * ab + sub].astype(jnp.float32)
        low = value.astype(jnp.bfloat16)
        from_x = 2 * (x_hi if sub else 1 - x_hi)
        for j, g in enumerate(groups(core, sub)):
            for i in (0, 1):
                for xl in (0, 1):
                    d1 = (1 - core) * (from_x + xl) + core * g
                    half = (1 - core) * j + core * i
                    spot = (1 - core) * i + core * xl
                    row = (2 * j + i) * HALF
                    s1[ab, d1, half, spot] = low[row : row + HALF, xl * 512 : xl * 512 + WIDE]

    def remote1(src_ref, ab, k, to):
        return pltpu.make_async_remote_copy(
            src_ref=src_ref, dst_ref=r1.at[ab, k], send_sem=s1_send.at[ab, k], recv_sem=s1_recv.at[ab, k],
            device_id=first(side(to)), device_id_type=MESH)

    def opposite(ab, to):
        return remote1(s1.at[ab, (me1 + 2) % 4, to], ab, to, to)

    def plain(ab, to):
        return remote1(s1.at[ab, side(to), 1 - to], ab, 2 + to, to)

    def relayed(ab, to):
        return remote1(joined.at[ab, to], ab, 4 + to, to)

    def relay(ab, to):
        opposite(ab, to).wait_recv()
        for j in (0, 1):
            joined[ab, to, j] = (
                s1[ab, side(to), to, j].astype(jnp.float32) + r1[ab, to, j].astype(jnp.float32)
            ).astype(jnp.bfloat16)
        relayed(ab, to).start()

    def s2_copy(ab, d2, slot):
        return pltpu.make_async_remote_copy(
            src_ref=s2.at[ab, d2], dst_ref=r2.at[ab, slot], send_sem=s2_send.at[ab, d2], recv_sem=s2_recv.at[ab, slot],
            device_id=second(d2), device_id_type=MESH)

    def second_stage(ab):
        for half in (0, 1):
            relayed(ab, half).wait_recv()
            plain(ab, 1 - half).wait_recv()
            for j in (0, 1):
                d2 = 2 * half + j
                total = (
                    s1[ab, me1, half, j].astype(jnp.float32)
                    + r1[ab, 4 + half, j].astype(jnp.float32)
                    + r1[ab, 3 - half, j].astype(jnp.float32)
                )
                s2[ab, d2] = total.astype(jnp.bfloat16)

                @pl.when(d2 == me2)
                def _():
                    mine[ab] = total

                @pl.when(d2 != me2)
                def _():
                    s2_copy(ab, d2, (me2 - d2 + 7) % 4 % 3).start()

    def collected(ab):
        for slot in range(3):
            s2_copy(ab, 0, slot).wait_recv()
        total = mine[ab]
        for slot in range(3):
            total = total + r2[ab, slot].astype(jnp.float32)
        return total

    def out_first(ab):
        opposite(ab, to1).start()
        opposite(ab, to2).start()
        plain(ab, to1).start()

    for_partner(0, 0)
    for_partner(0, 1)
    for_self(0, 0)
    out_first(0)
    for_partner(1, 0)
    for_self(0, 1)
    plain(0, to2).start()
    relay(0, to1)
    relay(0, to2)
    for_partner(1, 1)
    for_self(1, 0)
    out_first(1)
    for_self(1, 1)
    plain(1, to2).start()
    second_stage(0)
    relay(1, to1)
    relay(1, to2)
    early = collected(0)
    second_stage(1)
    total = jnp.concatenate([early, collected(1)], axis=0)

    pad = jnp.zeros((32, 128), jnp.float32)
    for tile in range(5):
        turned[tile * 128 : (tile + 1) * 128] = jnp.concatenate([total[:, tile * 128 : (tile + 1) * 128], pad], axis=0).T
    turned[WIDE:] = jnp.zeros((16, 128), jnp.float32)

    def s3_copy(k, c):
        zz = (z + k) % 8
        return pltpu.make_async_remote_copy(
            src_ref=s3.at[zz, c], dst_ref=r3.at[core, z], send_sem=s3_send.at[k, c], recv_sem=s3_recv.at[core, z],
            device_id=device(x, y, zz, c), device_id_type=MESH)

    for k in (4, 3, 5, 2, 6, 1, 7, 0):
        zz = (z + k) % 8
        for c in (0, 1):
            start = pl.multiple_of(64 * x_lo + 72 * zz + 32 * c, 8)
            s3[zz, c] = turned[pl.ds(start, MSG)].astype(jnp.bfloat16)
            if k > 0:
                s3_copy(k, c).start()
            else:

                @pl.when(core != c)
                def _():
                    s3_copy(k, c).start()

    r3[core, z] = s3[z, core]
    for k in range(8):
        zz = (z + k) % 8
        for c in (0, 1):

            def arrival():
                return pltpu.make_async_remote_copy(
                    src_ref=s3.at[0, 0], dst_ref=r3.at[c, zz], send_sem=s3_send.at[0, 0], recv_sem=s3_recv.at[c, zz],
                    device_id=device(x, y, z, 1 - core), device_id_type=MESH)

            if k > 0:
                arrival().wait_recv()
            else:

                @pl.when(core != c)
                def _():
                    arrival().wait_recv()

    fill = jnp.zeros((128 - MSG, 128), jnp.float32)
    for r in (0, 1):
        piece = r3[r, 0].astype(jnp.float32)
        for zz in range(1, 8):
            piece = piece + r3[r, zz].astype(jnp.float32)
        back = jnp.concatenate([piece, fill], axis=0).T
        out_ref[r] = jnp.where(core == 0, back[:ROWS, :36], back[:ROWS, 4:40])

    for ab in (0, 1):
        for sub in (0, 1):
            p_copy(ab, sub).wait_send()
            opposite(ab, sub).wait_send()
            plain(ab, sub).wait_send()
            relayed(ab, sub).wait_send()
        for d2 in range(4):

            @pl.when(d2 != me2)
            def _():
                s2_copy(ab, d2, 0).wait_send()

    for k in range(8):
        for c in (0, 1):
            if k > 0:
                s3_copy(k, c).wait_send()
            else:

                @pl.when(core != c)
                def _():
                    s3_copy(k, c).wait_send()


def local(integrals, bra_rows, ket_rows, block_count, pair_count):
    bf16, f32 = jnp.bfloat16, jnp.float32
    out = pl.pallas_call(
        kernel,
        out_shape=jax.ShapeDtypeStruct((2, ROWS, 36), f32),
        in_specs=[
            pl.BlockSpec(memory_space=pl.ANY),
            pl.BlockSpec(memory_space=pltpu.VMEM),
            pl.BlockSpec(memory_space=pltpu.VMEM),
            pl.BlockSpec(memory_space=pltpu.SMEM),
            pl.BlockSpec(memory_space=pltpu.SMEM),
        ],
        out_specs=pl.BlockSpec(memory_space=pltpu.VMEM),
        scratch_shapes=[
            pltpu.VMEM((NBLK * DEPTH, VW), bf16),
            pltpu.VMEM((2, 16, 128), f32),
            pltpu.VMEM((2, 48, 128), f32),
            pltpu.VMEM((2, 2, 4, ROWS, NBLK * DEPTH), bf16),
            pltpu.VMEM((4, 2 * ROWS, VW), bf16),
            pltpu.VMEM((4, 2 * ROWS, VW), bf16),
            pltpu.VMEM((2, 4, 2, 2, HALF, WIDE), bf16),
            pltpu.VMEM((2, 6, 2, HALF, WIDE), bf16),
            pltpu.VMEM((2, 2, 2, HALF, WIDE), bf16),
            pltpu.VMEM((2, 4, HALF, WIDE), bf16),
            pltpu.VMEM((2, 3, HALF, WIDE), bf16),
            pltpu.VMEM((2, HALF, WIDE), f32),
            pltpu.VMEM((WIDE + 16, 128), f32),
            pltpu.VMEM((8, 2, MSG, 128), bf16),
            pltpu.VMEM((2, 8, MSG, 128), bf16),
            pltpu.SemaphoreType.DMA((NBLK,)),
            pltpu.SemaphoreType.DMA((4,)),
            pltpu.SemaphoreType.DMA((4,)),
            pltpu.SemaphoreType.DMA((2, 6)),
            pltpu.SemaphoreType.DMA((2, 6)),
            pltpu.SemaphoreType.DMA((2, 4)),
            pltpu.SemaphoreType.DMA((2, 3)),
            pltpu.SemaphoreType.DMA((8, 2)),
            pltpu.SemaphoreType.DMA((2, 8)),
        ],
        compiler_params=pltpu.CompilerParams(
            collective_id=0, has_side_effects=True, vmem_limit_bytes=56 * 1024 * 1024
        ),
        name="transform",
    )(integrals.reshape(NBLK * DEPTH, VW), jnp.swapaxes(bra_rows, 2, 3), jnp.swapaxes(ket_rows, 2, 3), block_count, pair_count)
    return out.reshape(2, 4, 24, 36)


def solution(mesh):
    split = ("ao", "gen", "act")
    in_specs = (
        P(split, None, None, None),
        P(split, None, None, None),
        P(split, None, None, None),
        P(split),
        P(split),
    )
    out_specs = P(None, "gen", "act", "ao")
    return jax.shard_map(local, mesh=mesh, in_specs=in_specs, out_specs=out_specs, check_vma=False)
```

time: 54.7 us -> 46.9 us (0.86)
  local copies, waits for them, and re-layouts: 5.73 us -> 1.54 us
  Pallas kernels: 48.1 us -> 44.6 us
    unnamed x3 -> x1, local copies, waits for them, and re-layouts: 5.73 us -> 1.54 us
    pallas_call x1, Pallas kernels: 48.1 us -> 44.6 us  [local(): pl.pallas_call(kernel, out_shape=jax.ShapeDtypeStruct((2, ROWS, 36), f32)...]
where the time goes in v3:
time: 46.9 us; the launch traced here: 46.8 us
  Pallas kernels  44.6 us (95%)
  local copies, waits for them, and re-layouts  1.54 us (3%)
  between operations  0.66 us (1%)
    pallas_call x1, Pallas kernels, local(): pl.pallas_call(kernel, out_shape=jax.ShapeDtypeStruct((2, ROWS, 36), f32)...  44.6 us
    unnamed x1, local copies, waits for them, and re-layouts  1.54 us

profile of v3, /device:TPU:1, one launch (start us, length us, event | category | flops | bytes accessed | tf_op | source)
XLA Modules:
  0.0 46.8 jit_solution(805413723104287866)
XLA Ops:
  0.7 44.6 %transform.1 = f32[2,96,36]{2,1,0:T(8,128)} custom-call(bf16[3072,1152]{1,0:T(8,128)(2,1)} %bitcast.4, bf16[12,2,16,128]{3,2,1,0:T(8,128)(2,1)} %bitcast.7, bf16[12,2,48,128]{3,2,1,0:T(8,128)(2,1)} %bitcast.6, s32[1]{0:T(128)S(6)} %copy.7.block_count, s32[12]{0:T(128)} %pair_count.1), custom_call_target="tpu_custom_call" | custom-call | tf_op jit(solution)/shard_map/transform/pallas_call | solution.py:293
  45.2 1.5 %copy.8 = f32[2,4,24,36]{3,2,1,0:T(8,128)} copy(f32[2,4,24,36]{3,2,1,0:T(8,128)} %bitcast.5) | data formatting | bytes 55296

commit v4 on v2

--- a/solution.py
+++ b/solution.py
@@ -11,12 +11,12 @@
 VW = 1152
 ROWS = 96
 WIDE = 640
-MSG = 48
-
-
-def kernel(ints_hbm, bra_ref, ket_ref, block_count, pair_count, out_ref,
-           ints, bra_wide, ket_wide, weights, psend, precv, s1, r1, joined, s2, r2, mine, turned, s3, r3,
-           load_sem, p_send, p_recv, s1_send, s1_recv, s2_send, s2_recv, s3_send, s3_recv):
+MSG = 40
+
+
+def kernel(ints_hbm, bra_hbm, ket_hbm, block_count, pair_count, out_ref,
+           ints, acc, bra_ref, ket_ref, bra_wide, ket_wide, weights, psend, precv, s1, r1, joined, s2, r2, mine, turned, s3, r3,
+           small_sem, load_sem, p_send, p_recv, s1_send, s1_recv, s2_send, s2_recv, s3_send, s3_recv):
     ao, gen, act = lax.axis_index("ao"), lax.axis_index("gen"), lax.axis_index("act")
     core = ao % 2
     z = (ao // 2) % 8
@@ -37,11 +37,18 @@
     me1 = (1 - core) * x + core * y
     me2 = (1 - core) * y + core * x
 
+    small = [
+        pltpu.make_async_copy(bra_hbm, bra_ref, small_sem.at[0]),
+        pltpu.make_async_copy(ket_hbm, ket_ref, small_sem.at[1]),
+    ]
+    for copy in small:
+        copy.start()
     loads = []
     for b in range(NBLK):
         rows = pl.ds(b * DEPTH, DEPTH)
         loads.append(pltpu.make_async_copy(ints_hbm.at[rows], ints.at[rows], load_sem.at[b]))
-        loads[-1].start()
+    for copy in loads[: NBLK // 2]:
+        copy.start()
 
     barrier = pltpu.get_barrier_semaphore()
     pl.semaphore_signal(barrier, inc=1, device_id=device(x, y, z, 1 - core), device_id_type=MESH)
@@ -83,21 +90,24 @@
                 weights[1, yy * 2 + xh, :, high] = re_low
         return carry
 
-    lax.fori_loop(0, NBLK, build, 0)
-
-    for copy in loads:
+    for copy in small:
         copy.wait()
+    lax.fori_loop(0, NBLK // 2, build, 0)
+    for copy in loads[NBLK // 2 :]:
+        copy.start()
+    lax.fori_loop(NBLK // 2, NBLK, build, 0)
 
     other_x = 1 - x_hi
 
-    def chunk_of(part, t):
-        from_x = (other_x if t < 2 else x_hi) * 2 + t % 2
-        from_y = (y + (2, 1, 3, 0)[t]) % 4
-        return (1 - part) * from_x + part * from_y
-
-    def product(part, chunk):
-        lhs = weights[part, pl.ds(chunk * 2, 2)].reshape(2 * ROWS, NBLK * DEPTH)
-        return jnp.dot(lhs, ints[...], preferred_element_type=jnp.float32)
+    def groups(part, t):
+        from_x = (other_x if t < 2 else x_hi) * 4 + 2 * (t % 2)
+        near, far = (y + 1) % 4, (y + 3) % 4
+        pairs = (((y + 2) % 4, 0), ((y + 2) % 4, 1)), ((near, 0), (far, 0)), ((near, 1), (far, 1)), ((y, 0), (y, 1))
+        return [(1 - part) * (from_x + j) + part * (pairs[t][j][0] * 2 + pairs[t][j][1]) for j in (0, 1)]
+
+    def product(part, t, depth=slice(None)):
+        lhs = jnp.concatenate([weights[part, g, :, depth] for g in groups(part, t)], axis=0)
+        return jnp.dot(lhs, ints[depth], preferred_element_type=jnp.float32)
 
     def p_copy(t):
         return pltpu.make_async_remote_copy(
@@ -105,9 +115,17 @@
             device_id=device(x, y, z, 1 - core), device_id_type=MESH)
 
     def for_partner(t):
-        psend[t] = product(1 - core, chunk_of(1 - core, t)).astype(jnp.bfloat16)
         if t == 0:
+            middle = NBLK * DEPTH // 2
+            for copy in loads[: NBLK // 2]:
+                copy.wait()
+            acc[...] = product(1 - core, t, slice(0, middle))
+            for copy in loads[NBLK // 2 :]:
+                copy.wait()
+            psend[t] = (acc[...] + product(1 - core, t, slice(middle, None))).astype(jnp.bfloat16)
             pl.semaphore_wait(barrier, 21)
+        else:
+            psend[t] = product(1 - core, t).astype(jnp.bfloat16)
         p_copy(t).start()
 
     right, left = (me1 + 1) % 4, (me1 + 3) % 4
@@ -135,13 +153,15 @@
 
     def for_self(t):
         p_copy(t).wait_recv()
-        value = product(core, chunk_of(core, t)) + precv[t].astype(jnp.float32)
+        value = product(core, t) + precv[t].astype(jnp.float32)
         low = value.astype(jnp.bfloat16)
-        for j in (0, 1):
+        from_x = 2 * (other_x if t < 2 else x_hi)
+        for j, g in enumerate(groups(core, t)):
             for xl in (0, 1):
-                d1 = (1 - core) * (2 * (other_x if t < 2 else x_hi) + xl) + core * chunk_of(1, t)
-                d2 = (1 - core) * (2 * (t % 2) + j) + core * (2 * j + xl)
-                s1[d1, d2 // 2, d2 % 2] = low[j * ROWS : (j + 1) * ROWS, xl * 512 : xl * 512 + WIDE]
+                d1 = (1 - core) * (from_x + xl) + core * (g // 2)
+                half = (1 - core) * (t % 2) + core * (g % 2)
+                spot = (1 - core) * j + core * xl
+                s1[d1, half, spot] = low[j * ROWS : (j + 1) * ROWS, xl * 512 : xl * 512 + WIDE]
 
     is_y = core == 1
     even = jnp.logical_and(core == 0, x_lo == 0)
@@ -173,33 +193,42 @@
     def _():
         opposite(1).start()
 
+    @when(is_y)
+    def _():
+        plain(1).start()
+
+    @when(odd)
+    def _():
+        plain(0).start()
+
+    for_partner(3)
+
     @when(is_y, odd)
     def _():
+        relay(0)
+
+    for_self(2)
+
+    @when(is_y)
+    def _():
         plain(0).start()
+        relay(1)
+
+    @when(odd)
+    def _():
+        plain(1).start()
+
+    @when(even)
+    def _():
         relay(0)
 
-    for_partner(3)
-    for_self(2)
-
-    @when(is_y, odd)
-    def _():
-        plain(1).start()
+    for_self(3)
 
     @when(even)
     def _():
-        relay(0)
-
-    @when(is_y, even)
-    def _():
-        relay(1)
-
-    for_self(3)
-
-    @when(even)
-    def _():
         plain(0).start()
 
-    @when(odd)
+    @when(even, odd)
     def _():
         relay(1)
 
@@ -310,14 +339,17 @@
         out_shape=jax.ShapeDtypeStruct((2, ROWS, 36), f32),
         in_specs=[
             pl.BlockSpec(memory_space=pl.ANY),
-            pl.BlockSpec(memory_space=pltpu.VMEM),
-            pl.BlockSpec(memory_space=pltpu.VMEM),
+            pl.BlockSpec(memory_space=pl.ANY),
+            pl.BlockSpec(memory_space=pl.ANY),
             pl.BlockSpec(memory_space=pltpu.SMEM),
             pl.BlockSpec(memory_space=pltpu.SMEM),
         ],
         out_specs=pl.BlockSpec(memory_space=pltpu.VMEM),
         scratch_shapes=[
             pltpu.VMEM((NBLK * DEPTH, VW), bf16),
+            pltpu.VMEM((2 * ROWS, VW), f32),
+            pltpu.VMEM((NBLK, 2, 16, 128), bf16),
+            pltpu.VMEM((NBLK, 2, 48, 128), bf16),
             pltpu.VMEM((2, 16, 128), f32),
             pltpu.VMEM((2, 48, 128), f32),
             pltpu.VMEM((2, 8, ROWS, NBLK * DEPTH), bf16),
@@ -332,6 +364,7 @@
             pltpu.VMEM((WIDE + 16, 128), f32),
             pltpu.VMEM((8, 2, MSG, 128), bf16),
             pltpu.VMEM((2, 8, MSG, 128), bf16),
+            pltpu.SemaphoreType.DMA((2,)),
             pltpu.SemaphoreType.DMA((NBLK,)),
             pltpu.SemaphoreType.DMA((4,)),
             pltpu.SemaphoreType.DMA((4,)),
@@ -343,7 +376,7 @@
             pltpu.SemaphoreType.DMA((2, 8)),
         ],
         compiler_params=pltpu.CompilerParams(
-            collective_id=0, has_side_effects=True, vmem_limit_bytes=56 * 1024 * 1024
+            collective_id=0, has_side_effects=True, vmem_limit_bytes=63 * 1024 * 1024
         ),
         name="transform",
     )(integrals.reshape(NBLK * DEPTH, VW), jnp.swapaxes(bra_rows, 2, 3), jnp.swapaxes(ket_rows, 2, 3), block_count, pair_count)

time: 46.3 us -> 45.9 us (level)
  the two profiles are of different devices: /device:TPU:29 before, /device:TPU:17 now
where the time goes in v4:
time: 45.9 us; the launch traced here: 45.8 us
  Pallas kernels  43.6 us (95%)
  local copies, waits for them, and re-layouts  1.54 us (3%)
  between operations  0.66 us (1%)
    pallas_call x1, Pallas kernels, local(): pl.pallas_call(kernel, out_shape=jax.ShapeDtypeStruct((2, ROWS, 36), f32)...  43.6 us
    unnamed x1, local copies, waits for them, and re-layouts  1.54 us

profile of v4, /device:TPU:17, one launch (start us, length us, event | category | flops | bytes accessed | tf_op | source)
XLA Modules:
  0.0 45.8 jit_solution(14419103331230676300)
XLA Ops:
  0.7 43.6 %transform.1 = f32[2,96,36]{2,1,0:T(8,128)} custom-call(bf16[3072,1152]{1,0:T(8,128)(2,1)} %bitcast.4, bf16[12,2,16,128]{3,2,1,0:T(8,128)(2,1)} %bitcast.7, bf16[12,2,48,128]{3,2,1,0:T(8,128)(2,1)} %bitcast.6, s32[1]{0:T(128)S(6)} %copy.7.block_count, s32[12]{0:T(128)} %pair_count.1), custom_call_target="tpu_custom_call" | custom-call | tf_op jit(solution)/shard_map/transform/pallas_call | solution.py:337
  44.2 1.5 %copy.8 = f32[2,4,24,36]{3,2,1,0:T(8,128)} copy(f32[2,4,24,36]{3,2,1,0:T(8,128)} %bitcast.5) | data formatting | bytes 55296
